TPU v7x, 32 devices: a whole 2x2x4 slice. The times are simulated.
32 devices in a mesh: lat: 2 (over core), lon: 4 (over y, x), lev: 4 (over z).
Axes of the slice: x: 2, y: 2, z: 4, core: 2. Of those that a mesh axis runs over, the one named last changes fastest.
Arguments:
- field_values: float32 [16, 512, 64, 128], P('lat', 'lon', 'lev'), may hold values from 0.2 to 1.8
- crowding: float32 [16, 512, 64, 128], P('lat', 'lon', 'lev'), may hold values from 0.5 to 2
Outputs:
- potential: float32 [16, 512, 64, 128], P('lat', 'lon', 'lev')
- field_values_end: float32 [16, 512, 64, 128], P('lat', 'lon', 'lev')
All inputs are finite; a program needn't handle non-finite values.
Results may differ from a plain program's by a relative error of at most 0.00002.
Values sent between devices are 32-bit elements; how exact they have to be, the bound alone decides.
A program may use at most 256 MiB of HBM per device.

v0:
```python
import jax
import jax.numpy as jnp
from jax import lax
from jax.sharding import PartitionSpec as P

STEPS = 4


def with_halo(cells, sides, width):
    for axis, dim in sides:
        count = lax.axis_size(axis)
        head = lax.slice_in_dim(cells, 0, width, axis=dim)
        tail = lax.slice_in_dim(cells, cells.shape[dim] - width, cells.shape[dim], axis=dim)
        cells = jnp.concatenate(
            [
                lax.ppermute(tail, axis, [(i, (i + 1) % count) for i in range(count)]),
                cells,
                lax.ppermute(head, axis, [((i + 1) % count, i) for i in range(count)]),
            ],
            axis=dim,
        )
    return cells


def entering(part, axis, combine, identity):
    place = lax.axis_index(axis)
    gathered = lax.all_gather(part, axis)
    state = jnp.zeros_like(part) + jnp.asarray(identity, part.dtype)

    def one(turn, state):
        return combine(state, lax.dynamic_index_in_dim(gathered, turn, 0, False))

    return lax.fori_loop(0, place, one, state)


def without_rim(values, dims):
    for dim in dims:
        values = lax.slice_in_dim(values, 1, values.shape[dim] - 1, axis=dim)
    return values


def shifted_cells(values, dim, start, dims):
    others = [other for other in dims if other != dim]
    values = without_rim(values, others)
    return lax.slice_in_dim(values, start, start + values.shape[dim] - 2, axis=dim)


def march_step(padded, crowding):
    middle = without_rim(padded, (0, 1, 2))
    lower = [shifted_cells(padded, dim, 0, (0, 1, 2)) for dim in (0, 1, 2)]
    upper = [shifted_cells(padded, dim, 2, (0, 1, 2)) for dim in (0, 1, 2)]
    spread = lower[0] + upper[0] + lower[1] + upper[1] + lower[2] + upper[2] - 6.0 * middle
    return middle + 0.1 * spread + 0.2 * middle * (1.0 - middle * crowding)


def per_device(field_values, crowding):
    for step in range(STEPS):
        padded = with_halo(field_values, (("lat", 0), ("lon", 1), ("lev", 2)), 1)
        field_values = march_step(padded, crowding)
    here = jnp.cumsum(field_values, axis=2)
    total = lax.slice_in_dim(here, here.shape[2] - 1, here.shape[2], axis=2)

    def add_pair(earlier_total, later_total):
        return earlier_total + later_total

    below = entering(total, "lev", add_pair, jnp.zeros_like(total))
    potential = (here + below) / (field_values.shape[2] * lax.axis_size("lev"))
    return (potential, field_values)


def solution(mesh):
    return jax.shard_map(
        per_device,
        mesh=mesh,
        in_specs=(P("lat", "lon", "lev", None), P("lat", "lon", "lev", None)),
        out_specs=(P("lat", "lon", "lev", None), P("lat", "lon", "lev", None)),
        check_vma=False,
    )
```

profile of v0, /device:TPU:24, one launch (start us, length us, event | category | flops | bytes accessed | tf_op | source)
XLA Modules:
  0.0 361.4 jit_solution(2941315530111769444)
XLA Ops:
  7.2 1.7 fusion.42
  9.5 2.1 collective-permute-done
  11.7 4.0 %constant_dynamic-update-slice_fusion.1 = f32[10,128,16,128]{3,2,1,0:T(8,128)S(1)} fusion(f32[10,128,16,128]{3,2,1,0:T(8,128)S(1)} %constant_dynamic-update-slice_fusion.2, f32[8,128,16,128]{3,2,1,0:T(8,128)} %param.4), kind=kLoop, calls=%fused_computation.132 | loop fusion | bytes 16777216
  15.8 1.5 collective-permute-start.2
  18.8 2.9 collective-permute-done.2
  24.6 3.4 collective-permute-start.4
  28.1 16.4 %collective-permute-done.5 = f32[10,130,1,128]{3,1,2,0:T(8,128)S(1)} collective-permute-done((f32[10,130,1,128]{3,1,2,0:T(8,128)S(1)}, f32[10,130,1,128]{3,1,2,0:T(8,128)S(1)}, u32[]{:S(2)}, u32[]{:S(2)}) %collective-permute-start.5) | collective-permute-done | bytes 665632 | tf_op jit(solution)/shard_map/ppermute | solution.py:18
  45.1 11.0 %collective-permute-done.4 = f32[10,130,1,128]{3,1,2,0:T(8,128)S(1)} collective-permute-done((f32[10,130,1,128]{3,1,2,0:T(8,128)S(1)}, f32[10,130,1,128]{3,1,2,0:T(8,128)S(1)}, u32[]{:S(2)}, u32[]{:S(2)}) %collective-permute-start.4) | collective-permute-done | bytes 665632 | tf_op jit(solution)/shard_map/ppermute | solution.py:16
  56.8 24.4 %fusion.31 = f32[8,128,16,128]{3,2,1,0:T(8,128)S(1)} fusion(f32[8,128,16,128]{3,2,1,0:T(8,128)} %param.4, f32[10,130,1,128]{3,2,1,0:T(1,128)S(1)} %copy.26, f32[10,1,16,128]{3,2,1,0:T(8,128)S(1)} %collective-permute-done.3, f32[10,128,16,128]{3,2,1,0:T(8,128)} %copy-done.2, f32[10,1,16,128]{3,2,1,0:T(8,128)S(1)} %collective-permute-done.2, ...), kind=kLoop, calls=%fused_computation.87 | loop fusion | flops 50331648 | bytes 39243776 | tf_op jit(solution)/shard_map/add | solution.py:53
  81.9 2.1 collective-permute-done.6
  84.1 1.5 collective-permute-done.7
  85.6 1.8 collective-permute-start.8
  88.6 3.3 collective-permute-done.8
  92.0 1.9 pad_maximum_fusion.78
  94.6 3.6 collective-permute-start.10
  98.2 16.2 %collective-permute-done.11 = f32[10,130,1,128]{3,1,2,0:T(8,128)S(1)} collective-permute-done((f32[10,130,1,128]{3,1,2,0:T(8,128)S(1)}, f32[10,130,1,128]{3,1,2,0:T(8,128)S(1)}, u32[]{:S(2)}, u32[]{:S(2)}) %collective-permute-start.11) | collective-permute-done | bytes 665632 | tf_op jit(solution)/shard_map/ppermute | solution.py:18
  114.4 1.5 copy.30
  115.9 11.0 %collective-permute-done.10 = f32[10,130,1,128]{3,1,2,0:T(8,128)S(1)} collective-permute-done((f32[10,130,1,128]{3,1,2,0:T(8,128)S(1)}, f32[10,130,1,128]{3,1,2,0:T(8,128)S(1)}, u32[]{:S(2)}, u32[]{:S(2)}) %collective-permute-start.10) | collective-permute-done | bytes 665632 | tf_op jit(solution)/shard_map/ppermute | solution.py:16
  126.9 1.5 copy.28
  128.5 16.0 %fusion.22 = f32[8,128,16,128]{3,2,1,0:T(8,128)} fusion(f32[8,128,16,128]{3,2,1,0:T(8,128)S(1)} %fusion.31, f32[10,130,1,128]{3,2,1,0:T(1,128)} %copy.30, f32[10,1,16,128]{3,2,1,0:T(8,128)S(1)} %collective-permute-done.9, f32[10,1,16,128]{3,2,1,0:T(8,128)S(1)} %collective-permute-done.8, f32[1,128,16,128]{3,2,1,0:T(8,128)} %copy-done.3, ...), kind=kLoop, calls=%fused_computation.60 | loop fusion | flops 67108864 | bytes 28758016 | tf_op jit(solution)/shard_map/add | solution.py:53
  144.5 1.8 fusion.40
  146.9 2.1 collective-permute-done.12
  151.5 1.6 collective-permute-start.14
  154.5 3.1 collective-permute-done.14
  158.4 1.9 pad_maximum_fusion.73
  161.9 2.5 collective-permute-start.16
  164.4 16.4 %collective-permute-done.17 = f32[10,130,1,128]{3,1,2,0:T(8,128)S(1)} collective-permute-done((f32[10,130,1,128]{3,1,2,0:T(8,128)S(1)}, f32[10,130,1,128]{3,1,2,0:T(8,128)S(1)}, u32[]{:S(2)}, u32[]{:S(2)}) %collective-permute-start.17) | collective-permute-done | bytes 665632 | tf_op jit(solution)/shard_map/ppermute | solution.py:18
  180.8 1.5 copy.34
  182.3 11.2 %collective-permute-done.16 = f32[10,130,1,128]{3,1,2,0:T(8,128)S(1)} collective-permute-done((f32[10,130,1,128]{3,1,2,0:T(8,128)S(1)}, f32[10,130,1,128]{3,1,2,0:T(8,128)S(1)}, u32[]{:S(2)}, u32[]{:S(2)}) %collective-permute-start.16) | collective-permute-done | bytes 665632 | tf_op jit(solution)/shard_map/ppermute | solution.py:16
  193.5 1.5 copy.32
  195.1 16.0 %fusion.13 = f32[8,128,16,128]{3,2,1,0:T(8,128)} fusion(f32[8,128,16,128]{3,2,1,0:T(8,128)S(1)} %copy-done, f32[10,130,1,128]{3,2,1,0:T(1,128)} %copy.34, f32[10,1,16,128]{3,2,1,0:T(8,128)S(1)} %collective-permute-done.15, f32[10,1,16,128]{3,2,1,0:T(8,128)S(1)} %collective-permute-done.14, f32[1,128,16,128]{3,2,1,0:T(8,128)} %copy-done.4, ...), kind=kLoop, calls=%fused_computation.33 | loop fusion | flops 67108864 | bytes 28758016 | tf_op jit(solution)/shard_map/add | solution.py:53
  211.1 1.8 fusion.39
  213.5 2.1 collective-permute-done.18
  218.1 1.8 collective-permute-start.20
  221.1 3.3 collective-permute-done.20
  225.0 1.9 pad_maximum_fusion.68
  228.1 3.1 collective-permute-start.22
  231.1 16.2 %collective-permute-done.23 = f32[10,130,1,128]{3,1,2,0:T(8,128)S(1)} collective-permute-done((f32[10,130,1,128]{3,1,2,0:T(8,128)S(1)}, f32[10,130,1,128]{3,1,2,0:T(8,128)S(1)}, u32[]{:S(2)}, u32[]{:S(2)}) %collective-permute-start.23) | collective-permute-done | bytes 665632 | tf_op jit(solution)/shard_map/ppermute | solution.py:18
  247.4 1.5 copy.38
  248.9 11.6 %collective-permute-done.22 = f32[10,130,1,128]{3,1,2,0:T(8,128)S(1)} collective-permute-done((f32[10,130,1,128]{3,1,2,0:T(8,128)S(1)}, f32[10,130,1,128]{3,1,2,0:T(8,128)S(1)}, u32[]{:S(2)}, u32[]{:S(2)}) %collective-permute-start.22) | collective-permute-done | bytes 665632 | tf_op jit(solution)/shard_map/ppermute | solution.py:16
  260.5 1.6 copy.36
  262.0 16.0 %fusion.4 = f32[8,128,16,128]{3,2,1,0:T(8,128)} fusion(f32[8,128,16,128]{3,2,1,0:T(8,128)S(1)} %copy-done.1, f32[10,130,1,128]{3,2,1,0:T(1,128)} %copy.38, f32[10,1,16,128]{3,2,1,0:T(8,128)S(1)} %collective-permute-done.21, f32[10,1,16,128]{3,2,1,0:T(8,128)S(1)} %collective-permute-done.20, f32[1,128,16,128]{3,2,1,0:T(8,128)} %copy-done.5, ...), kind=kLoop, calls=%fused_computation.6 | loop fusion | flops 67108864 | bytes 28758016 | tf_op jit(solution)/shard_map/add | solution.py:53
  278.0 11.6 %fusion.36 = f32[8,128,16,128]{3,1,2,0:T(8,128)} fusion(f32[8,128,16,128]{3,2,1,0:T(8,128)} %fusion.4), kind=kOutput, calls=%fused_computation.101 | output fusion | flops 31457280 | bytes 16777216 | tf_op jit(solution)/shard_map/jit(cumsum)/reduce_window_sum | solution.py:60
  289.7 1.9 slice.360
  291.6 44.8 %all-gather.3.cloned.1.call-done = f32[32,128,1,128]{3,1,2,0:T(8,128)} async-done(((f32[8,128,1,128]{3,1,2,0:T(8,128)}), f32[32,128,1,128]{3,1,2,0:T(8,128)}) %all-gather.3.cloned.1.call-update) | async-done | bytes 2097168 | tf_op jit(solution)/shard_map/all_gather | solution.py:27
  336.6 5.3 %while.10 = (s32[]{:T(128)}, f32[8,128,1,128]{3,2,1,0:T(1,128)S(1)}, s32[]{:T(128)}, f32[4,8,128,1,128]{4,2,1,3,0:T(8,128)}, s32[]{:T(128)}, /*index=5*/s32[]{:T(128)}, s32[]{:T(128)}) while((s32[]{:T(128)}, f32[8,128,1,128]{3,2,1,0:T(1,128)S(1)}, s32[]{:T(128)}, f32[4,8,128,1,128]{4,2,1,3,0:T(8,128)}, s32[]{:T(128)}, /*index=5*/s32[]{:T(128)}, ...), condition=%wide.region_2.3_spmd, body=%wide.region_1.2_spmd.sunk | while | flops 131077 | bytes 2621563 | solution.py:33
  342.0 4.4 %add_multiply_fusion = f32[8,128,16,128]{3,1,2,0:T(8,128)S(1)} fusion(f32[8,128,16,128]{3,1,2,0:T(8,128)} %fusion.36, f32[8,128,128]{2,1,0:T(8,128)S(1)} %bitcast.8), kind=kLoop, calls=%fused_computation.103 | loop fusion | flops 4194304 | bytes 17301504 | tf_op jit(solution)/shard_map/div | solution.py:67
  346.4 8.1 %copy.41 = f32[8,128,16,128]{3,2,1,0:T(8,128)} copy(f32[8,128,16,128]{3,1,2,0:T(8,128)S(1)} %add_multiply_fusion) | data formatting | bytes 16777216
  (62 shorter events, 27.2 us)
Async XLA Ops:
  7.2 329.2 %all-gather.3.cloned.1.call-start = ((), (), s32[]{:S(2)}) async-start(), calls=%async_computation | async-start | bytes 2621440 | tf_op jit(solution)/shard_map/all_gather | solution.py:27
  8.9 2.7 collective-permute-start
  9.0 6.7 %collective-permute-start.1 = (f32[1,128,16,128]{3,2,1,0:T(8,128)S(1)}, f32[1,128,16,128]{3,2,1,0:T(8,128)S(1)}, u32[]{:S(2)}, u32[]{:S(2)}) collective-permute-start(f32[1,128,16,128]{3,2,1,0:T(8,128)S(1)} %get-tuple-element.74), channel_id=1, source_target_pairs={{16,0},{0,16},{17,1},{1,17},{18,2},{2,18},{19,3},{3,19},{20,4},{4,... | collective-permute-start | bytes 3145736 | tf_op jit(solution)/shard_map/ppermute | solution.py:18
  15.8 40.3 %copy-start.2 = (f32[10,128,16,128]{3,2,1,0:T(8,128)}, f32[10,128,16,128]{3,2,1,0:T(8,128)S(1)}, u32[]{:S(2)}) copy-start(f32[10,128,16,128]{3,2,1,0:T(8,128)S(1)} %constant_dynamic-update-slice_fusion) | copy-start | bytes 31457284
  15.8 5.9 %collective-permute-start.2 = (f32[10,1,16,128]{3,2,1,0:T(8,128)S(1)}, f32[10,1,16,128]{3,2,1,0:T(8,128)S(1)}, u32[]{:S(2)}, u32[]{:S(2)}) collective-permute-start(f32[10,1,16,128]{3,2,1,0:T(8,128)S(1)} %get-tuple-element.66), channel_id=1, source_target_pairs={{0,4},{4,8},{8,12},{12,0},{1,5},{5,9},{9,13},{13,1},{2,6},{6,10},{... | collective-permute-start | bytes 245768 | tf_op jit(solution)/shard_map/ppermute | solution.py:16
  17.4 5.7 %collective-permute-start.3 = (f32[10,1,16,128]{3,2,1,0:T(8,128)S(1)}, f32[10,1,16,128]{3,2,1,0:T(8,128)S(1)}, u32[]{:S(2)}, u32[]{:S(2)}) collective-permute-start(f32[10,1,16,128]{3,2,1,0:T(8,128)S(1)} %get-tuple-element.67), channel_id=1, source_target_pairs={{4,0},{8,4},{12,8},{0,12},{5,1},{9,5},{13,9},{1,13},{6,2},{10,6},{... | collective-permute-start | bytes 245768 | tf_op jit(solution)/shard_map/ppermute | solution.py:18
  24.1 20.3 %collective-permute-start.5 = (f32[10,130,1,128]{3,1,2,0:T(8,128)S(1)}, f32[10,130,1,128]{3,1,2,0:T(8,128)S(1)}, u32[]{:S(2)}, u32[]{:S(2)}) collective-permute-start(f32[10,130,1,128]{3,1,2,0:T(8,128)S(1)} %copy.25), channel_id=1, source_target_pairs={{1,0},{2,1},{3,2},{0,3},{5,4},{6,5},{7,6},{4,7},{9,8},{10,9},{11,1... | collective-permute-start | bytes 1996808 | tf_op jit(solution)/shard_map/ppermute | solution.py:18
  24.6 31.5 %collective-permute-start.4 = (f32[10,130,1,128]{3,1,2,0:T(8,128)S(1)}, f32[10,130,1,128]{3,1,2,0:T(8,128)S(1)}, u32[]{:S(2)}, u32[]{:S(2)}) collective-permute-start(f32[10,130,1,128]{3,1,2,0:T(8,128)S(1)} %copy.23), channel_id=1, source_target_pairs={{0,1},{1,2},{2,3},{3,0},{4,5},{5,6},{6,7},{7,4},{8,9},{9,10},{10,1... | collective-permute-start | bytes 1996808 | tf_op jit(solution)/shard_map/ppermute | solution.py:16
  81.3 2.7 collective-permute-start.6
  81.4 4.1 %collective-permute-start.7 = (f32[1,128,16,128]{3,2,1,0:T(8,128)S(1)}, f32[1,128,16,128]{3,2,1,0:T(8,128)S(1)}, u32[]{:S(2)}, u32[]{:S(2)}) collective-permute-start(f32[1,128,16,128]{3,2,1,0:T(8,128)S(1)} %get-tuple-element.73), channel_id=1, source_target_pairs={{16,0},{0,16},{17,1},{1,17},{18,2},{2,18},{19,3},{3,19},{20,4},{4,... | collective-permute-start | bytes 3145736 | tf_op jit(solution)/shard_map/ppermute | solution.py:18
  85.6 8.4 %copy-start.3 = (f32[1,128,16,128]{3,2,1,0:T(8,128)}, f32[1,128,16,128]{3,2,1,0:T(8,128)S(1)}, u32[]{:S(2)}) copy-start(f32[1,128,16,128]{3,2,1,0:T(8,128)S(1)} %collective-permute-done.7) | copy-start | bytes 3145732
  85.6 6.3 %collective-permute-start.8 = (f32[10,1,16,128]{3,2,1,0:T(8,128)S(1)}, f32[10,1,16,128]{3,2,1,0:T(8,128)S(1)}, u32[]{:S(2)}, u32[]{:S(2)}) collective-permute-start(f32[10,1,16,128]{3,2,1,0:T(8,128)S(1)} %get-tuple-element.64), channel_id=1, source_target_pairs={{0,4},{4,8},{8,12},{12,0},{1,5},{5,9},{9,13},{13,1},{2,6},{6,10},{... | collective-permute-start | bytes 245768 | tf_op jit(solution)/shard_map/ppermute | solution.py:16
  87.4 4.7 %collective-permute-start.9 = (f32[10,1,16,128]{3,2,1,0:T(8,128)S(1)}, f32[10,1,16,128]{3,2,1,0:T(8,128)S(1)}, u32[]{:S(2)}, u32[]{:S(2)}) collective-permute-start(f32[10,1,16,128]{3,2,1,0:T(8,128)S(1)} %get-tuple-element.65), channel_id=1, source_target_pairs={{4,0},{8,4},{12,8},{0,12},{5,1},{9,5},{13,9},{1,13},{6,2},{10,6},{... | collective-permute-start | bytes 245768 | tf_op jit(solution)/shard_map/ppermute | solution.py:18
  94.0 20.4 %collective-permute-start.11 = (f32[10,130,1,128]{3,1,2,0:T(8,128)S(1)}, f32[10,130,1,128]{3,1,2,0:T(8,128)S(1)}, u32[]{:S(2)}, u32[]{:S(2)}) collective-permute-start(f32[10,130,1,128]{3,1,2,0:T(8,128)S(1)} %copy.29), channel_id=1, source_target_pairs={{1,0},{2,1},{3,2},{0,3},{5,4},{6,5},{7,6},{4,7},{9,8},{10,9},{11,1... | collective-permute-start | bytes 1996808 | tf_op jit(solution)/shard_map/ppermute | solution.py:18
  94.6 32.4 %collective-permute-start.10 = (f32[10,130,1,128]{3,1,2,0:T(8,128)S(1)}, f32[10,130,1,128]{3,1,2,0:T(8,128)S(1)}, u32[]{:S(2)}, u32[]{:S(2)}) collective-permute-start(f32[10,130,1,128]{3,1,2,0:T(8,128)S(1)} %copy.27), channel_id=1, source_target_pairs={{0,1},{1,2},{2,3},{3,0},{4,5},{5,6},{6,7},{7,4},{8,9},{9,10},{10,1... | collective-permute-start | bytes 1996808 | tf_op jit(solution)/shard_map/ppermute | solution.py:16
  144.5 14.0 %copy-start = (f32[8,128,16,128]{3,2,1,0:T(8,128)S(1)}, f32[8,128,16,128]{3,2,1,0:T(8,128)}, u32[]{:S(2)}) copy-start(f32[8,128,16,128]{3,2,1,0:T(8,128)} %fusion.22) | copy-start | bytes 25165828
  146.3 2.7 collective-permute-start.12
  146.4 4.1 %collective-permute-start.13 = (f32[1,128,16,128]{3,2,1,0:T(8,128)S(1)}, f32[1,128,16,128]{3,2,1,0:T(8,128)S(1)}, u32[]{:S(2)}, u32[]{:S(2)}) collective-permute-start(f32[1,128,16,128]{3,2,1,0:T(8,128)S(1)} %get-tuple-element.71), channel_id=1, source_target_pairs={{16,0},{0,16},{17,1},{1,17},{18,2},{2,18},{19,3},{3,19},{20,4},{4,... | collective-permute-start | bytes 3145736 | tf_op jit(solution)/shard_map/ppermute | solution.py:18
  150.5 9.8 %copy-start.4 = (f32[1,128,16,128]{3,2,1,0:T(8,128)}, f32[1,128,16,128]{3,2,1,0:T(8,128)S(1)}, u32[]{:S(2)}) copy-start(f32[1,128,16,128]{3,2,1,0:T(8,128)S(1)} %collective-permute-done.13) | copy-start | bytes 3145732
  151.5 6.1 %collective-permute-start.14 = (f32[10,1,16,128]{3,2,1,0:T(8,128)S(1)}, f32[10,1,16,128]{3,2,1,0:T(8,128)S(1)}, u32[]{:S(2)}, u32[]{:S(2)}) collective-permute-start(f32[10,1,16,128]{3,2,1,0:T(8,128)S(1)} %get-tuple-element.62), channel_id=1, source_target_pairs={{0,4},{4,8},{8,12},{12,0},{1,5},{5,9},{9,13},{13,1},{2,6},{6,10},{... | collective-permute-start | bytes 245768 | tf_op jit(solution)/shard_map/ppermute | solution.py:16
  153.1 5.3 %collective-permute-start.15 = (f32[10,1,16,128]{3,2,1,0:T(8,128)S(1)}, f32[10,1,16,128]{3,2,1,0:T(8,128)S(1)}, u32[]{:S(2)}, u32[]{:S(2)}) collective-permute-start(f32[10,1,16,128]{3,2,1,0:T(8,128)S(1)} %get-tuple-element.63), channel_id=1, source_target_pairs={{4,0},{8,4},{12,8},{0,12},{5,1},{9,5},{13,9},{1,13},{6,2},{10,6},{... | collective-permute-start | bytes 245768 | tf_op jit(solution)/shard_map/ppermute | solution.py:18
  160.4 20.4 %collective-permute-start.17 = (f32[10,130,1,128]{3,1,2,0:T(8,128)S(1)}, f32[10,130,1,128]{3,1,2,0:T(8,128)S(1)}, u32[]{:S(2)}, u32[]{:S(2)}) collective-permute-start(f32[10,130,1,128]{3,1,2,0:T(8,128)S(1)} %copy.33), channel_id=1, source_target_pairs={{1,0},{2,1},{3,2},{0,3},{5,4},{6,5},{7,6},{4,7},{9,8},{10,9},{11,1... | collective-permute-start | bytes 1996808 | tf_op jit(solution)/shard_map/ppermute | solution.py:18
  161.9 31.6 %collective-permute-start.16 = (f32[10,130,1,128]{3,1,2,0:T(8,128)S(1)}, f32[10,130,1,128]{3,1,2,0:T(8,128)S(1)}, u32[]{:S(2)}, u32[]{:S(2)}) collective-permute-start(f32[10,130,1,128]{3,1,2,0:T(8,128)S(1)} %copy.31), channel_id=1, source_target_pairs={{0,1},{1,2},{2,3},{3,0},{4,5},{5,6},{6,7},{7,4},{8,9},{9,10},{10,1... | collective-permute-start | bytes 1996808 | tf_op jit(solution)/shard_map/ppermute | solution.py:16
  211.1 13.9 %copy-start.1 = (f32[8,128,16,128]{3,2,1,0:T(8,128)S(1)}, f32[8,128,16,128]{3,2,1,0:T(8,128)}, u32[]{:S(2)}) copy-start(f32[8,128,16,128]{3,2,1,0:T(8,128)} %fusion.13) | copy-start | bytes 25165828
  212.9 2.7 collective-permute-start.18
  213.0 4.1 %collective-permute-start.19 = (f32[1,128,16,128]{3,2,1,0:T(8,128)S(1)}, f32[1,128,16,128]{3,2,1,0:T(8,128)S(1)}, u32[]{:S(2)}, u32[]{:S(2)}) collective-permute-start(f32[1,128,16,128]{3,2,1,0:T(8,128)S(1)} %get-tuple-element.69), channel_id=1, source_target_pairs={{16,0},{0,16},{17,1},{1,17},{18,2},{2,18},{19,3},{3,19},{20,4},{4,... | collective-permute-start | bytes 3145736 | tf_op jit(solution)/shard_map/ppermute | solution.py:18
  217.1 9.7 %copy-start.5 = (f32[1,128,16,128]{3,2,1,0:T(8,128)}, f32[1,128,16,128]{3,2,1,0:T(8,128)S(1)}, u32[]{:S(2)}) copy-start(f32[1,128,16,128]{3,2,1,0:T(8,128)S(1)} %collective-permute-done.19) | copy-start | bytes 3145732
  218.1 6.3 %collective-permute-start.20 = (f32[10,1,16,128]{3,2,1,0:T(8,128)S(1)}, f32[10,1,16,128]{3,2,1,0:T(8,128)S(1)}, u32[]{:S(2)}, u32[]{:S(2)}) collective-permute-start(f32[10,1,16,128]{3,2,1,0:T(8,128)S(1)} %get-tuple-element.60), channel_id=1, source_target_pairs={{0,4},{4,8},{8,12},{12,0},{1,5},{5,9},{9,13},{13,1},{2,6},{6,10},{... | collective-permute-start | bytes 245768 | tf_op jit(solution)/shard_map/ppermute | solution.py:16
  219.9 5.0 %collective-permute-start.21 = (f32[10,1,16,128]{3,2,1,0:T(8,128)S(1)}, f32[10,1,16,128]{3,2,1,0:T(8,128)S(1)}, u32[]{:S(2)}, u32[]{:S(2)}) collective-permute-start(f32[10,1,16,128]{3,2,1,0:T(8,128)S(1)} %get-tuple-element.61), channel_id=1, source_target_pairs={{4,0},{8,4},{12,8},{0,12},{5,1},{9,5},{13,9},{1,13},{6,2},{10,6},{... | collective-permute-start | bytes 245768 | tf_op jit(solution)/shard_map/ppermute | solution.py:18
  226.9 20.4 %collective-permute-start.23 = (f32[10,130,1,128]{3,1,2,0:T(8,128)S(1)}, f32[10,130,1,128]{3,1,2,0:T(8,128)S(1)}, u32[]{:S(2)}, u32[]{:S(2)}) collective-permute-start(f32[10,130,1,128]{3,1,2,0:T(8,128)S(1)} %copy.37), channel_id=1, source_target_pairs={{1,0},{2,1},{3,2},{0,3},{5,4},{6,5},{7,6},{4,7},{9,8},{10,9},{11,1... | collective-permute-start | bytes 1996808 | tf_op jit(solution)/shard_map/ppermute | solution.py:18
  228.1 32.4 %collective-permute-start.22 = (f32[10,130,1,128]{3,1,2,0:T(8,128)S(1)}, f32[10,130,1,128]{3,1,2,0:T(8,128)S(1)}, u32[]{:S(2)}, u32[]{:S(2)}) collective-permute-start(f32[10,130,1,128]{3,1,2,0:T(8,128)S(1)} %copy.35), channel_id=1, source_target_pairs={{0,1},{1,2},{2,3},{3,0},{4,5},{5,6},{6,7},{7,4},{8,9},{9,10},{10,1... | collective-permute-start | bytes 1996808 | tf_op jit(solution)/shard_map/ppermute | solution.py:16
Sparse Core Ops, SparseCore 0:
  291.7 44.6 all-gather.2
where the time goes:
time: 362 us; the launch traced here: 361 us
  waiting for transfers between devices  183 us (51%)
  other arithmetic  98.8 us (27%)
  local copies, waits for them, and re-layouts  34.1 us (9%)
  starting transfers between devices  30.3 us (8%)
  between operations  14.3 us (4%)
    ppermute x12, waiting for transfers between devices, with_halo(): lax.ppermute(head, axis, [((i + 1) % count, i) for i in range(count)])  72.6 us
    add x4, other arithmetic, march_step(): return middle + 0.1 * spread + 0.2 * middle * (1.0 - middle * crowding)  72.4 us
    ppermute x12, waiting for transfers between devices, with_halo(): lax.ppermute(tail, axis, [(i, (i + 1) % count) for i in range(count)])  66 us
    all_gather x1, waiting for transfers between devices, entering(): gathered = lax.all_gather(part, axis)  44.8 us
    ppermute x12, starting transfers between devices, with_halo(): lax.ppermute(tail, axis, [(i, (i + 1) % count) for i in range(count)])  19.6 us
    unnamed x15, local copies, waits for them, and re-layouts  12.2 us
    another operation x1, other arithmetic, per_device(): here = jnp.cumsum(field_values, axis=2)  11.6 us
    ppermute x12, starting transfers between devices, with_halo(): lax.ppermute(head, axis, [((i + 1) % count, i) for i in range(count)])  10.7 us
  transfers between devices with their start and end apart: 25, of which 24 were waited for; matrix products, arithmetic and copies ran while one was open for 3% of the time, Pallas kernels for 0%

commit v1 on v0

v1 whole, which is shorter than its diff:
```python
import functools

import jax
import jax.numpy as jnp
from jax import lax
from jax.experimental import pallas as pl
from jax.experimental.pallas import tpu as pltpu
from jax.sharding import PartitionSpec as P

STEPS = 4
BLOCK = 8


def row_order(rows):
    order = []
    for k in range((rows + 1) // 2):
        order.append(k)
        if rows - 1 - k != k:
            order.append(rows - 1 - k)
    return order


def kernel(
    sizes, f_hbm, c_hbm, pot_hbm, end_hbm,
    field, crowd, lat_lo, lat_hi, lon_lo, lon_hi, lev_lo, lev_hi, face_lo, face_hi, below, sums,
    in_sem, out_sem, lat_send, lat_recv, lon_send, lon_recv, lev_send, lev_recv, sum_send, sum_recv,
):
    Y, X, Z, L = crowd.shape
    order = row_order(Y)
    levels_at = lax.axis_index("lev")
    last = sizes["lev"] - 1
    scale = 1.0 / (Z * sizes["lev"])

    def beside(axis, shift):
        n = sizes[axis]
        return {axis: lax.rem(lax.axis_index(axis) + (shift + n), n)}

    def send(src, dst, send_sem, recv_sem, axis, shift):
        return pltpu.make_async_remote_copy(
            src_ref=src, dst_ref=dst, send_sem=send_sem, recv_sem=recv_sem,
            device_id=beside(axis, shift), device_id_type=pl.DeviceIdType.MESH,
        )

    f_in = [pltpu.make_async_copy(f_hbm.at[y], field.at[0, y, pl.ds(0, X)], in_sem.at[0, y]) for y in range(Y)]
    c_in = [pltpu.make_async_copy(c_hbm.at[y], crowd.at[y], in_sem.at[1, y]) for y in range(Y)]
    for y in order:
        f_in[y].start()
    for y in order:
        c_in[y].start()

    barrier = pltpu.get_barrier_semaphore()
    for axis in ("lat", "lon", "lev"):
        for shift in (-1, 1):
            pl.semaphore_signal(barrier, inc=1, device_id=beside(axis, shift), device_id_type=pl.DeviceIdType.MESH)
    pl.semaphore_wait(barrier, 6)

    def lev_copies(t, y):
        return [
            send(face_lo.at[t, y], lev_hi.at[t, y], lev_send.at[0, t, y], lev_recv.at[0, t, y], "lev", -1),
            send(face_hi.at[t, y], lev_lo.at[t, y], lev_send.at[1, t, y], lev_recv.at[1, t, y], "lev", 1),
        ]

    def lon_copies(t, y):
        row = field.at[t % 2, y]
        return [
            send(row.at[0], lon_hi.at[t, y], lon_send.at[0, t, y], lon_recv.at[0, t, y], "lon", -1),
            send(row.at[X - 1], lon_lo.at[t, y], lon_send.at[1, t, y], lon_recv.at[1, t, y], "lon", 1),
        ]

    def lat_low(t):
        return send(field.at[t % 2, 0, pl.ds(0, X)], lat_hi.at[t], lat_send.at[0, t], lat_recv.at[0, t], "lat", -1)

    def lat_high(t):
        return send(field.at[t % 2, Y - 1, pl.ds(0, X)], lat_lo.at[t], lat_send.at[1, t], lat_recv.at[1, t], "lat", 1)

    def send_row(t, y):
        for copy in lev_copies(t, y) + lon_copies(t, y):
            copy.start()
        if y == 0:
            lat_low(t).start()
        if y == Y - 1:
            lat_high(t).start()

    def sum_copy(y):
        return send(sums.at[y], below.at[y], sum_send.at[y], sum_recv.at[y], "lev", 1)

    for y in order:
        f_in[y].wait()

        @pl.loop(0, X // BLOCK)
        def _(at):
            base = pl.multiple_of(at * BLOCK, BLOCK)
            for i in range(BLOCK):
                face_lo[0, y, pl.ds(base + i, 1), :] = field[0, y, base + i, 0:1, :]
                face_hi[0, y, pl.ds(base + i, 1), :] = field[0, y, base + i, Z - 1 : Z, :]

        send_row(0, y)

    place = lax.broadcasted_iota(jnp.int32, (Z, L), 0)

    for t in range(STEPS):
        now, later = t % 2, (t + 1) % 2
        if t >= 1:
            for y in order:
                for copy in lon_copies(t - 1, y):
                    copy.wait_send()
            lat_low(t - 1).wait_send()
            lat_high(t - 1).wait_send()
        for y in order:
            if t == 0:
                c_in[y].wait()
            if y == 0:
                lat_high(t).wait_recv()
            if y == Y - 1:
                lat_low(t).wait_recv()
            for copy in lon_copies(t, y) + lev_copies(t, y):
                copy.wait_recv()
            before = field.at[now, y - 1] if y > 0 else lat_lo.at[t]
            after = field.at[now, y + 1] if y < Y - 1 else lat_hi.at[t]
            field[now, y, X] = lon_hi[t, y]

            def block(at, carry):
                left, middle = carry
                base = pl.multiple_of(at * BLOCK, BLOCK)
                for i in range(BLOCK):
                    x = base + i
                    right = field[now, y, x + 1]
                    lower = jnp.where(place == 0, lev_lo[t, y, pl.ds(x, 1), :], pltpu.roll(middle, 1, 0))
                    upper = jnp.where(place == Z - 1, lev_hi[t, y, pl.ds(x, 1), :], pltpu.roll(middle, Z - 1, 0))
                    around = (left + right) + (before[x] + after[x]) + (lower + upper)
                    new = 0.1 * around + middle * (0.6 - 0.2 * (middle * crowd[y, x]))
                    field[later, y, x] = new
                    if t < STEPS - 1:
                        face_lo[t + 1, y, pl.ds(x, 1), :] = new[0:1]
                        face_hi[t + 1, y, pl.ds(x, 1), :] = new[Z - 1 : Z]
                    else:
                        shift = 1
                        while shift < Z:
                            new = new + jnp.where(place >= shift, pltpu.roll(new, shift, 0), 0.0)
                            shift *= 2
                        crowd[y, x] = new
                        sums[y, pl.ds(x, 1), :] = new[Z - 1 : Z]
                    left, middle = middle, right
                return left, middle

            lax.fori_loop(0, X // BLOCK, block, (lon_lo[t, y], field[now, y, 0]))
            if t < STEPS - 1:
                send_row(t + 1, y)
            else:
                pltpu.make_async_copy(field.at[later, y, pl.ds(0, X)], end_hbm.at[y], out_sem.at[0, y]).start()

                @pl.when(levels_at == 0)
                def _():
                    sum_copy(y).start()

    @pl.when(levels_at == 0)
    def _():
        below[...] = jnp.zeros_like(below)

    for y in order:
        @pl.when(levels_at > 0)
        def _():
            sum_copy(y).wait_recv()

            @pl.when(levels_at < last)
            def _():
                sums[y] = sums[y] + below[y]
                sum_copy(y).start()

        @pl.loop(0, X // BLOCK)
        def _(at):
            base = pl.multiple_of(at * BLOCK, BLOCK)
            for i in range(BLOCK):
                x = base + i
                crowd[y, x] = (crowd[y, x] + below[y, pl.ds(x, 1), :]) * scale

        pltpu.make_async_copy(crowd.at[y], pot_hbm.at[y], out_sem.at[1, y]).start()

    for y in order:
        @pl.when(levels_at < last)
        def _():
            sum_copy(y).wait_send()

        pltpu.make_async_copy(field.at[STEPS % 2, y, pl.ds(0, X)], end_hbm.at[y], out_sem.at[0, y]).wait()
        pltpu.make_async_copy(crowd.at[y], pot_hbm.at[y], out_sem.at[1, y]).wait()
        for t in range(STEPS):
            for copy in lev_copies(t, y):
                copy.wait_send()
        for copy in lon_copies(STEPS - 1, y):
            copy.wait_send()
    lat_low(STEPS - 1).wait_send()
    lat_high(STEPS - 1).wait_send()


def per_device(sizes, field_values, crowding):
    Y, X, Z, L = field_values.shape
    f32 = jnp.float32
    dma = pltpu.SemaphoreType.DMA
    anywhere = pl.BlockSpec(memory_space=pl.ANY)
    shape = jax.ShapeDtypeStruct(field_values.shape, f32)
    return pl.pallas_call(
        functools.partial(kernel, sizes),
        out_shape=(shape, shape),
        in_specs=[anywhere, anywhere],
        out_specs=(anywhere, anywhere),
        scratch_shapes=[
            pltpu.VMEM((2, Y, X + 1, Z, L), f32),
            pltpu.VMEM((Y, X, Z, L), f32),
            pltpu.VMEM((STEPS, X, Z, L), f32),
            pltpu.VMEM((STEPS, X, Z, L), f32),
            pltpu.VMEM((STEPS, Y, Z, L), f32),
            pltpu.VMEM((STEPS, Y, Z, L), f32),
            pltpu.VMEM((STEPS, Y, X, L), f32),
            pltpu.VMEM((STEPS, Y, X, L), f32),
            pltpu.VMEM((STEPS, Y, X, L), f32),
            pltpu.VMEM((STEPS, Y, X, L), f32),
            pltpu.VMEM((Y, X, L), f32),
            pltpu.VMEM((Y, X, L), f32),
            dma((2, Y)),
            dma((2, Y)),
            dma((2, STEPS)),
            dma((2, STEPS)),
            dma((2, STEPS, Y)),
            dma((2, STEPS, Y)),
            dma((2, STEPS, Y)),
            dma((2, STEPS, Y)),
            dma((Y,)),
            dma((Y,)),
        ],
        compiler_params=pltpu.CompilerParams(
            collective_id=0, has_side_effects=True, vmem_limit_bytes=60 * 1024 * 1024
        ),
    )(field_values, crowding)


def solution(mesh):
    return jax.shard_map(
        functools.partial(per_device, dict(mesh.shape)),
        mesh=mesh,
        in_specs=(P("lat", "lon", "lev", None), P("lat", "lon", "lev", None)),
        out_specs=(P("lat", "lon", "lev", None), P("lat", "lon", "lev", None)),
        check_vma=False,
    )
```

time: 362 us -> 128 us (0.35)
  waiting for transfers between devices: 183 us -> 0 us
  Pallas kernels: 0 us -> 116 us
  other arithmetic: 98.8 us -> 0 us
  starting transfers between devices: 30.3 us -> 0 us
  local copies, waits for them, and re-layouts: 34.1 us -> 11.1 us
  between operations: 14.3 us -> 0.65 us
    ppermute x24 -> x0, waiting for transfers between devices: 139 us -> none  [the longest x12 72.6 us: with_halo(): lax.ppermute(head, axis, [((i + 1) % count, i) for i in range(count)])]
    pallas_call x0 -> x1, Pallas kernels: none -> 116 us  [per_device(): pl.pallas_call(functools.partial(kernel, sizes), out_shape=(shape, shape)...]
    add x7 -> x0, other arithmetic: 74.1 us -> none  [the longest x4 72.4 us: march_step(): return middle + 0.1 * spread + 0.2 * middle * (1.0 - middle * crowding)]
    all_gather x1 -> x0, waiting for transfers between devices: 44.8 us -> none  [entering(): gathered = lax.all_gather(part, axis)]
    ppermute x24 -> x0, starting transfers between devices: 30.3 us -> none  [the longest x12 19.6 us: with_halo(): lax.ppermute(tail, axis, [(i, (i + 1) % count) for i in range(count)])]
    another operation x1 -> x0, other arithmetic: 11.6 us -> none  [per_device(): here = jnp.cumsum(field_values, axis=2)]
    ppermute x8 -> x0, local copies, waits for them, and re-layouts: 10.6 us -> none  [the longest x4 5.32 us: with_halo(): lax.ppermute(tail, axis, [(i, (i + 1) % count) for i in range(count)])]
    slice x7 -> x0, other arithmetic: 8.7 us -> none  [with_halo(): lax.slice_in_dim(cells, cells.shape[dim] - width, cells.shape[dim], axis=...]
  transfers between devices with their start and end apart: 25 -> 0, of which waited for: 24 -> 0; matrix products, arithmetic and copies ran while one was open for 3% -> 0% of each run, Pallas kernels for 0% -> 0%
where the time goes in v1:
time: 128 us; the launch traced here: 127 us
  Pallas kernels  116 us (91%)
  local copies, waits for them, and re-layouts  11.1 us (9%)
    pallas_call x1, Pallas kernels, per_device(): pl.pallas_call(functools.partial(kernel, sizes), out_shape=(shape, shape)...  116 us
    unnamed x4, local copies, waits for them, and re-layouts  11.1 us

profile of v1, /device:TPU:24, one launch (start us, length us, event | category | flops | bytes accessed | tf_op | source)
XLA Modules:
  0.0 127.5 jit_solution(15941542342593254168)
XLA Ops:
  0.6 115.7 %shard_map.41 = (f32[8,128,16,128]{3,2,1,0:T(8,128)}, f32[8,128,16,128]{3,2,1,0:T(8,128)}) custom-call(f32[8,128,16,128]{3,2,1,0:T(8,128)} %f_hbm.1, f32[8,128,16,128]{3,2,1,0:T(8,128)} %c_hbm.1), custom_call_target="tpu_custom_call" | custom-call | tf_op jit(solution)/shard_map/pallas_call | solution.py:201
  116.4 0.0 copy-start
  116.4 7.7 %copy.6 = f32[8,128,16,128]{3,2,1,0:T(8,128)} copy(f32[8,128,16,128]{3,2,1,0:T(8,128)} %get-tuple-element.4) | data formatting | bytes 16777216
  124.1 0.0 copy-done
  124.1 3.4 %copy.7 = f32[8,128,16,128]{3,2,1,0:T(8,128)} copy(f32[8,128,16,128]{3,2,1,0:T(8,128)S(1)} %copy-done) | data formatting | bytes 16777216
Async XLA Ops:
  116.4 7.7 %copy-start = (f32[8,128,16,128]{3,2,1,0:T(8,128)S(1)}, f32[8,128,16,128]{3,2,1,0:T(8,128)}, u32[]{:S(2)}) copy-start(f32[8,128,16,128]{3,2,1,0:T(8,128)} %get-tuple-element.5) | copy-start | bytes 25165828

commit v2 on v1

--- a/solution.py
+++ b/solution.py
@@ -21,7 +21,7 @@
 
 
 def kernel(
-    sizes, f_hbm, c_hbm, pot_hbm, end_hbm,
+    sizes, f_hbm, c_hbm, end_hbm, below_hbm,
     field, crowd, lat_lo, lat_hi, lon_lo, lon_hi, lev_lo, lev_hi, face_lo, face_hi, below, sums,
     in_sem, out_sem, lat_send, lat_recv, lon_send, lon_recv, lev_send, lev_recv, sum_send, sum_recv,
 ):
@@ -29,7 +29,6 @@
     order = row_order(Y)
     levels_at = lax.axis_index("lev")
     last = sizes["lev"] - 1
-    scale = 1.0 / (Z * sizes["lev"])
 
     def beside(axis, shift):
         n = sizes[axis]
@@ -134,12 +133,7 @@
                         face_lo[t + 1, y, pl.ds(x, 1), :] = new[0:1]
                         face_hi[t + 1, y, pl.ds(x, 1), :] = new[Z - 1 : Z]
                     else:
-                        shift = 1
-                        while shift < Z:
-                            new = new + jnp.where(place >= shift, pltpu.roll(new, shift, 0), 0.0)
-                            shift *= 2
-                        crowd[y, x] = new
-                        sums[y, pl.ds(x, 1), :] = new[Z - 1 : Z]
+                        sums[y, pl.ds(x, 1), :] = jnp.sum(new, axis=0, keepdims=True)
                     left, middle = middle, right
                 return left, middle
 
@@ -167,14 +161,7 @@
                 sums[y] = sums[y] + below[y]
                 sum_copy(y).start()
 
-        @pl.loop(0, X // BLOCK)
-        def _(at):
-            base = pl.multiple_of(at * BLOCK, BLOCK)
-            for i in range(BLOCK):
-                x = base + i
-                crowd[y, x] = (crowd[y, x] + below[y, pl.ds(x, 1), :]) * scale
-
-        pltpu.make_async_copy(crowd.at[y], pot_hbm.at[y], out_sem.at[1, y]).start()
+        pltpu.make_async_copy(below.at[y], below_hbm.at[y], out_sem.at[1, y]).start()
 
     for y in order:
         @pl.when(levels_at < last)
@@ -182,7 +169,7 @@
             sum_copy(y).wait_send()
 
         pltpu.make_async_copy(field.at[STEPS % 2, y, pl.ds(0, X)], end_hbm.at[y], out_sem.at[0, y]).wait()
-        pltpu.make_async_copy(crowd.at[y], pot_hbm.at[y], out_sem.at[1, y]).wait()
+        pltpu.make_async_copy(below.at[y], below_hbm.at[y], out_sem.at[1, y]).wait()
         for t in range(STEPS):
             for copy in lev_copies(t, y):
                 copy.wait_send()
@@ -192,15 +179,33 @@
     lat_high(STEPS - 1).wait_send()
 
 
+def finish(scale, end_ref, below_ref, pot_ref, copy_ref):
+    _, X, Z, L = end_ref.shape
+    place = lax.broadcasted_iota(jnp.int32, (Z, L), 0)
+
+    @pl.loop(0, X // BLOCK)
+    def _(at):
+        base = pl.multiple_of(at * BLOCK, BLOCK)
+        for i in range(BLOCK):
+            x = base + i
+            here = end_ref[0, x]
+            copy_ref[0, x] = here
+            shift = 1
+            while shift < Z:
+                here = here + jnp.where(place >= shift, pltpu.roll(here, shift, 0), 0.0)
+                shift *= 2
+            pot_ref[0, x] = (here + below_ref[0, pl.ds(x, 1), :]) * scale
+
+
 def per_device(sizes, field_values, crowding):
     Y, X, Z, L = field_values.shape
     f32 = jnp.float32
     dma = pltpu.SemaphoreType.DMA
     anywhere = pl.BlockSpec(memory_space=pl.ANY)
     shape = jax.ShapeDtypeStruct(field_values.shape, f32)
-    return pl.pallas_call(
+    end, below = pl.pallas_call(
         functools.partial(kernel, sizes),
-        out_shape=(shape, shape),
+        out_shape=(shape, jax.ShapeDtypeStruct((Y, X, L), f32)),
         in_specs=[anywhere, anywhere],
         out_specs=(anywhere, anywhere),
         scratch_shapes=[
@@ -231,6 +236,15 @@
             collective_id=0, has_side_effects=True, vmem_limit_bytes=60 * 1024 * 1024
         ),
     )(field_values, crowding)
+    width = X // 2
+    cells = pl.BlockSpec((1, width, Z, L), lambda y, x: (y, x, 0, 0))
+    return pl.pallas_call(
+        functools.partial(finish, 1.0 / (Z * sizes["lev"])),
+        grid=(Y, X // width),
+        out_shape=(shape, shape),
+        in_specs=[cells, pl.BlockSpec((1, width, L), lambda y, x: (y, x, 0))],
+        out_specs=(cells, cells),
+    )(end, below)
 
 
 def solution(mesh):

time: 128 us -> 132 us (1.031)
  Pallas kernels: 116 us -> 130 us
  local copies, waits for them, and re-layouts: 11.1 us -> 0 us
    pallas_call x1 -> x2, Pallas kernels: 116 us -> 130 us  [the longest x1 115 us: per_device(): pl.pallas_call(functools.partial(kernel, sizes), out_shape=(shape, jax.Sh...]
    unnamed x4 -> x0, local copies, waits for them, and re-layouts: 11.1 us -> none
where the time goes in v2:
time: 132 us; the launch traced here: 131 us
  Pallas kernels  130 us (98%)
    pallas_call x1, Pallas kernels, per_device(): pl.pallas_call(functools.partial(kernel, sizes), out_shape=(shape, jax.Sh...  115 us
    pallas_call x1, Pallas kernels, per_device(): pl.pallas_call(functools.partial(finish, 1.0 / (Z * sizes['lev'])), grid=...  15.2 us

profile of v2, /device:TPU:24, one launch (start us, length us, event | category | flops | bytes accessed | tf_op | source)
XLA Modules:
  0.0 131.1 jit_solution(1566128006490688640)
XLA Ops:
  0.6 115.2 %shard_map.41 = (f32[8,128,16,128]{3,2,1,0:T(8,128)}, f32[8,128,128]{2,1,0:T(8,128)}) custom-call(f32[8,128,16,128]{3,2,1,0:T(8,128)} %f_hbm.1, f32[8,128,16,128]{3,2,1,0:T(8,128)} %c_hbm.1), custom_call_target="tpu_custom_call" | custom-call | tf_op jit(solution)/shard_map/pallas_call | solution.py:206
  115.9 15.2 %shard_map.42 = (f32[8,128,16,128]{3,2,1,0:T(8,128)}, f32[8,128,16,128]{3,2,1,0:T(8,128)}) custom-call(f32[8,128,16,128]{3,2,1,0:T(8,128)} %get-tuple-element.4.end_ref, f32[8,128,128]{2,1,0:T(8,128)} %get-tuple-element.5.below_ref), custom_call_target="tpu_custom_call" | custom-call | tf_op jit(solution)/shard_map/pallas_call | solution.py:241
